TPU v7x, 32 devices: a whole 2x2x4 slice. The times are simulated.
32 devices in a mesh: curve: 8 (over z, y), sub: 4 (over x, core).
Axes of the slice: x: 2, y: 2, z: 4, core: 2. Of those that a mesh axis runs over, the one named last changes fastest.
Arguments:
- forcing: float32 [12, 768, 1024], P(None, 'curve', 'sub'), may hold values from -10 to 10
- metric: float32 [768, 1024], P('curve', 'sub'), may hold values from 0.25 to 4
- jacobian: float32 [768, 1024], P('curve', 'sub'), may hold values from 0.5 to 2
- mode_scale: float32 [12], replicated, may hold values from 0.1 to 10
Outputs:
- solution: float32 [12, 768, 1024], P(None, 'curve', 'sub')
- residual: float32 [12, 768, 1024], P(None, 'curve', 'sub')
All inputs are finite; a program needn't handle non-finite values.
Results may differ from a plain program's by a relative error of at most 0.0003.
Values sent between devices are 32-bit elements; how exact they have to be, the bound alone decides.
A program may use at most 64 MiB of HBM per device.

v0:
```python
import functools
import math

import jax
import jax.numpy as jnp
import numpy as np
from jax import lax
from jax.experimental import pallas as pl
from jax.experimental.pallas import tpu as pltpu
from jax.sharding import PartitionSpec as P

ITERS = 3
GROUPS = 2
UNROLL = True
MESH = pl.DeviceIdType.MESH
LANES = 128
f32 = jnp.float32
bf16 = jnp.bfloat16


def gll_tables():
    points = np.array([-1.0, -1.0 / math.sqrt(5.0), 1.0 / math.sqrt(5.0), 1.0])
    weights = np.array([1.0 / 6.0, 5.0 / 6.0, 5.0 / 6.0, 1.0 / 6.0])
    factor = np.array(
        [np.prod([points[j] - points[m] for m in range(4) if m != j]) for j in range(4)]
    )
    slopes = np.zeros((4, 4))
    for i in range(4):
        for j in range(4):
            if i != j:
                slopes[i, j] = factor[i] / (factor[j] * (points[i] - points[j]))
        slopes[i, i] = sum((1.0 / (points[i] - points[m]) for m in range(4) if m != i))
    return (slopes, weights)


SLOPES, WEIGHTS = gll_tables()


def combo(coefs, parts):
    total = None
    for c, v in zip(coefs, parts):
        if abs(c) < 1e-12:
            continue
        term = v * f32(c)
        total = term if total is None else total + term
    return total


def kernel(
    nc, ns, modes, groups,
    scale_hbm, forcing_ref, metric_ref, jac_ref, grad_hbm, div_hbm,
    x, r,
    z, d, s, w, invp, mass, flux, zcat, gout, sums, coef,
    row_tx, row_rx, col_tx, col_rx, cor_rx, ar_tx, ar_rx,
    source, factors, grad_ref, div_ref, scale_ref,
    htx_sem, hrx_sem, atx_sem, arx_sem, in_sem, table_sem,
):
    rows, cols = metric_ref.shape
    q = rows // 4
    n = nc * ns
    half = cols - LANES
    tiles = cols // LANES
    per = modes // groups
    slots = row_tx.shape[2]
    loads, sources = [], []
    for c in range(tiles):
        cut = pl.ds(c * LANES, LANES)
        loads += [
            pltpu.make_async_copy(jac_ref.at[:, cut], factors.at[0, c], in_sem.at[0, c]),
            pltpu.make_async_copy(metric_ref.at[:, cut], factors.at[1, c], in_sem.at[1, c]),
        ]
        sources.append(
            pltpu.make_async_copy(forcing_ref.at[:, :, cut], source.at[c], in_sem.at[2, c]))
    div_load = pltpu.make_async_copy(div_hbm, div_ref, table_sem.at[0])
    grad_load = pltpu.make_async_copy(grad_hbm, grad_ref, table_sem.at[1])
    scale_load = pltpu.make_async_copy(scale_hbm, scale_ref, table_sem.at[2])
    for copy in loads + sources + [div_load, scale_load, grad_load]:
        copy.start()

    me_c, me_s = lax.axis_index("curve"), lax.axis_index("sub")
    me = me_c * ns + me_s
    up, down = lax.rem(me_c + nc - 1, nc), lax.rem(me_c + 1, nc)
    left, right = lax.rem(me_s + ns - 1, ns), lax.rem(me_s + 1, ns)

    def place(offset):
        target = lax.rem(me + offset, n)
        return (target // ns, lax.rem(target, ns))

    barrier = pltpu.get_barrier_semaphore()

    def greet(offset, carry):
        pl.semaphore_signal(barrier, inc=1, device_id=place(offset), device_id_type=MESH)
        return carry

    lax.fori_loop(1, n, greet, 0)

    lane_full = lax.broadcasted_iota(jnp.int32, (q, cols), 1)
    lane = lax.broadcasted_iota(jnp.int32, (q, LANES), 1)
    row_at = lax.broadcasted_iota(jnp.int32, (q, cols), 0)
    phase = lane_full % 4
    on_edge = (phase == 0) | (phase == 3)
    take_next = (phase == 3) & (lane_full != cols - 1)
    take_prev = (phase == 0) & (lane_full != 0)

    def load(ref, m):
        return [ref[m, p * q:(p + 1) * q, :] for p in range(4)]

    def save(ref, m, parts):
        for p in range(4):
            ref[m, p * q:(p + 1) * q, :] = parts[p]

    def load2(ref):
        return [ref[p * q:(p + 1) * q, :] for p in range(4)]

    def pack(k, m, slot, h, tops):
        lo, hi = tops
        row_tx[k, 0, pl.ds(slot, 1), :] = h[0][0:1, :]
        row_tx[k, 1, pl.ds(slot, 1), :] = h[3][q - 1:q, :]
        t0 = h[0] + jnp.where(row_at == 0, 0.0, pltpu.roll(h[3], 1, 0))
        t3 = h[3] + jnp.where(row_at == q - 1, 0.0, pltpu.roll(h[0], q - 1, 0))
        t = [t0, h[1], h[2], t3]
        save(w, m, t)
        for p in range(4):
            at = 4 * slot + p
            lo = jnp.where(lane == at, pltpu.roll(t[p][:, :LANES], at, 1), lo)
            hi = jnp.where(lane == at, pltpu.roll(t[p][:, half:], at + 1, 1), hi)
        return lo, hi

    def halo_copies(k):
        plan = [
            (row_tx.at[k, 0], row_rx.at[k, 1], (up, me_s)),
            (row_tx.at[k, 1], row_rx.at[k, 0], (down, me_s)),
            (col_tx.at[k, 0, pl.ds(0, 1)], cor_rx.at[k, 3], (up, left)),
            (col_tx.at[k, 1, pl.ds(0, 1)], cor_rx.at[k, 2], (up, right)),
            (col_tx.at[k, 0, pl.ds(q - 1, 1)], cor_rx.at[k, 1], (down, left)),
            (col_tx.at[k, 1, pl.ds(q - 1, 1)], cor_rx.at[k, 0], (down, right)),
            (col_tx.at[k, 0], col_rx.at[k, 1], (me_c, left)),
            (col_tx.at[k, 1], col_rx.at[k, 0], (me_c, right)),
        ]
        return [
            pltpu.make_async_remote_copy(
                src_ref=src, dst_ref=dst, send_sem=htx_sem.at[k, e], recv_sem=hrx_sem.at[k, e],
                device_id=where, device_id_type=MESH)
            for e, (src, dst, where) in enumerate(plan)
        ]

    def send(k, tops):
        col_tx[k, 0], col_tx[k, 1] = tops
        for copy in halo_copies(k):
            copy.start()

    def arrive(k):
        for copy in halo_copies(k):
            copy.wait_recv()
        ph = lax.broadcasted_iota(jnp.int32, (1, LANES), 1) % 4
        edge_row = lax.broadcasted_iota(jnp.int32, (q, LANES), 0)
        merged = []
        for side in range(2):
            above, below = cor_rx[k, side], cor_rx[k, 2 + side]
            above = jnp.where(ph == 0, pltpu.roll(above, LANES - 3, 1), 0.0)
            below = jnp.where(ph == 3, pltpu.roll(below, 3, 1), 0.0)
            c = col_rx[k, side]
            c = c + jnp.where(edge_row == 0, above, 0.0) + jnp.where(edge_row == q - 1, below, 0.0)
            merged.append(c)
        return merged

    def assembled(k, m, slot, merged):
        t = load(w, m)
        t[0] = t[0] + jnp.where(row_at == 0, row_rx[k, 0, pl.ds(slot, 1), :], 0.0)
        t[3] = t[3] + jnp.where(row_at == q - 1, row_rx[k, 1, pl.ds(slot, 1), :], 0.0)
        out = []
        for p in range(4):
            at = 4 * slot + p
            c = t[p] + jnp.where(
                take_next, pltpu.roll(t[p], cols - 1, 1),
                jnp.where(take_prev, pltpu.roll(t[p], 1, 1), 0.0))
            a = jnp.where(lane == 0, pltpu.roll(merged[0], LANES - at, 1), 0.0)
            b = jnp.where(lane == LANES - 1, pltpu.roll(merged[1], LANES - 1 - at, 1), 0.0)
            pieces = [c[:, e * LANES:(e + 1) * LANES] for e in range(tiles)]
            pieces[0] = pieces[0] + a
            pieces[-1] = pieces[-1] + b
            out.append(jnp.concatenate(pieces, axis=1))
        return out

    edge_w, mid_w = f32(1.0 / 6.0), f32(5.0 / 6.0)
    col_w = jnp.where(on_edge, edge_w, mid_w)
    mw, fw = [], []
    for copy in loads:
        copy.wait()
    for p in range(4):
        grid_w = col_w * (edge_w if p in (0, 3) else mid_w)
        mw.append(strided([factors.at[0, c] for c in range(tiles)], p, q) * grid_w)
        fw.append(strided([factors.at[1, c] for c in range(tiles)], p, q) * grid_w)
        mass[p * q:(p + 1) * q, :] = mw[p]
        flux[p * q:(p + 1) * q, :] = fw[p]
    zero = jnp.zeros((q, LANES), f32)
    tops = pack(0, modes, per, mw, (zero, zero))
    div_load.wait()
    table = div_ref[:cols, :].astype(f32) + div_ref[2 * cols:, :].astype(f32)
    by_cols = jnp.dot(flux[...], table * table, precision=lax.Precision.HIGHEST,
                      preferred_element_type=f32)
    squared = SLOPES * SLOPES
    lap = [combo(squared[:, a], fw) + by_cols[a * q:(a + 1) * q, :] for a in range(4)]
    tops = pack(0, modes + 1, per + 1, lap, tops)
    for copy in sources:
        copy.wait()
    for g in range(groups):

        def start_body(slot, carry, g=g):
            m = g * per + slot
            h = [strided([source.at[c, m] for c in range(tiles)], p, q)
                 * mass[p * q:(p + 1) * q, :] for p in range(4)]
            return pack(g, m, slot, h, carry)

        tops = lax.fori_loop(0, per, start_body, tops if g == 0 else (zero, zero), unroll=UNROLL)
        if g == 0:
            pl.semaphore_wait(barrier, n - 1)
        send(g, tops)
    scale_load.wait()
    grad_load.wait()

    pad = (lax.broadcasted_iota(jnp.int32, (1, LANES), 1) >= per).astype(f32)
    eye = lax.broadcasted_iota(jnp.int32, (slots, LANES), 0) == lax.broadcasted_iota(
        jnp.int32, (slots, LANES), 1)

    def update(it, g, m, slot, ww):
        a, b = coef[g, 0, pl.ds(slot, 1), :], coef[g, 1, pl.ds(slot, 1), :]
        zz = load(z, m)
        if it > 1:
            dd, ss = load(d, m), load(s, m)
            zz = [u + b * v for u, v in zip(zz, dd)]
            ww = [u + b * v for u, v in zip(ww, ss)]
            xx = [u + a * v for u, v in zip(load(x, m), zz)]
        else:
            xx = [a * v for v in zz]
        rr = [u - a * v for u, v in zip(load(r, m), ww)]
        return zz, ww, xx, rr

    def fill(slot, parts):
        v = jnp.concatenate(parts, axis=0)
        top = v.astype(bf16)
        at = pl.ds(pl.multiple_of(slot * rows, rows), rows)
        zcat[at, :cols] = top
        zcat[at, cols:] = (v - top.astype(f32)).astype(bf16)

    def multiply(table_ref):
        gout[...] = (
            jnp.dot(zcat[...], table_ref[:2 * cols, :], preferred_element_type=f32)
            + jnp.dot(zcat[:, :cols], table_ref[2 * cols:, :], preferred_element_type=f32))

    old = [None] * groups

    def coefficients(it, g):
        k = it * groups + g
        gathered = ar_rx.at[k, pl.ds(1, n - 1)]
        pltpu.make_async_copy(gathered, gathered, arx_sem.at[k]).wait()
        total = jnp.sum(ar_rx[k], axis=0)
        rho, curve_sum = total[0:1] + pad, total[1:2] + pad
        if it == 0:
            mixing = jnp.zeros_like(rho)
            step_len = rho / curve_sum
        else:
            mixing = rho / old[g][0]
            step_len = rho / (curve_sum - mixing * rho / old[g][1])
        for e, line in enumerate((step_len, mixing)):
            tall = jnp.sum(jnp.where(eye, line, 0.0), axis=1, keepdims=True)
            coef[g, e] = jnp.broadcast_to(tall, (slots, cols))
        old[g] = (rho, step_len)

    for it in range(ITERS):
        for g in range(groups):
            base = g * per
            k = it * groups + g
            merged = arrive(k)
            if it == 0 and g == 0:
                for e in range(2):
                    save(w, modes + e, assembled(k, modes + e, per + e, merged))
            if it > 0:
                coefficients(it - 1, g)

            def first(slot, carry, it=it, g=g, k=k, base=base, merged=merged):
                m = base + slot
                ww = assembled(k, m, slot, merged)
                if it == 0:
                    rr = ww
                    inv = [1.0 / (u + scale_ref[m] * v)
                           for u, v in zip(load(w, modes), load(w, modes + 1))]
                    save(invp, m, inv)
                else:
                    dd, ss, xx, rr = update(it, g, m, slot, ww)
                    save(x, m, xx)
                    save(d, m, dd)
                    save(s, m, ss)
                    inv = load(invp, m)
                save(r, m, rr)
                zz = [u * v for u, v in zip(rr, inv)]
                save(z, m, zz)
                fill(slot, zz)
                rz = [u * v for u, v in zip(rr, zz)]
                rho = (rz[0] + rz[3]) * 0.5 + (rz[1] + rz[2])
                rho = jnp.where(on_edge, rho * 0.5, rho)
                sums[0, pl.ds(slot, 1), :] = jnp.sum(rho, axis=0, keepdims=True)
                f = load2(flux)
                fg = [f[a] * combo(SLOPES[a], zz) * scale_ref[m] for a in range(4)]
                ms = load2(mass)
                save(w, m, [ms[a] * zz[a] + combo(SLOPES[:, a], fg) for a in range(4)])
                return carry

            lax.fori_loop(0, per, first, 0, unroll=UNROLL)
            multiply(grad_ref)

            def second(slot, carry, base=base):
                grad = gout[pl.ds(pl.multiple_of(slot * rows, rows), rows), :]
                fill(slot, [flux[...] * grad * scale_ref[base + slot]])
                return carry

            lax.fori_loop(0, per, second, 0, unroll=UNROLL)
            multiply(div_ref)

            def third(slot, carry, k=k, base=base):
                m = base + slot
                zz = load(z, m)
                h = [u + gout[pl.ds(pl.multiple_of(slot * rows + p * q, q), q), :]
                     for p, u in enumerate(load(w, m))]
                zh = zz[0] * h[0] + zz[1] * h[1] + zz[2] * h[2] + zz[3] * h[3]
                sums[1, pl.ds(slot, 1), :] = jnp.sum(zh, axis=0, keepdims=True)
                return pack(k + groups, m, slot, h, carry)

            tops = lax.fori_loop(0, per, third, (zero, zero), unroll=UNROLL)
            send(k + groups, tops)
            for e in range(2):
                part = jnp.sum(sums[e], axis=1, keepdims=True)
                line = jnp.sum(jnp.where(eye, part, 0.0), axis=0, keepdims=True)
                ar_tx[k, e:e + 1, :] = line
                ar_rx[k, 0, e:e + 1, :] = line

            def spread(offset, carry, k=k):
                pltpu.make_async_remote_copy(
                    src_ref=ar_tx.at[k], dst_ref=ar_rx.at[k, offset],
                    send_sem=atx_sem.at[k], recv_sem=arx_sem.at[k],
                    device_id=place(offset), device_id_type=MESH).start()
                return carry

            lax.fori_loop(1, n, spread, 0, unroll=True if n <= 32 else 1)

    for g in range(groups):
        k = ITERS * groups + g
        merged = arrive(k)
        coefficients(ITERS - 1, g)

        def last(slot, carry, g=g, k=k, merged=merged):
            m = g * per + slot
            _, _, xx, rr = update(ITERS, g, m, slot, assembled(k, m, slot, merged))
            save(x, m, xx)
            save(r, m, rr)
            return carry

        lax.fori_loop(0, per, last, 0, unroll=UNROLL)

    for k in range((ITERS + 1) * groups):
        for copy in halo_copies(k):
            copy.wait_send()
    for k in range(ITERS * groups):
        sent = ar_rx.at[k, pl.ds(1, n - 1)]
        pltpu.make_async_copy(sent, sent, atx_sem.at[k]).wait()


def node_order(x, r, sol_ref, res_ref, sol_buf, res_buf, sem):
    modes, rows, cols = x.shape
    q, tiles = rows // 4, cols // LANES

    def stores(m):
        return [
            pltpu.make_async_copy(
                buf.at[c, m], out.at[m, :, pl.ds(c * LANES, LANES)], sem.at[k, c, m])
            for k, (buf, out) in enumerate(((sol_buf, sol_ref), (res_buf, res_ref)))
            for c in range(tiles)
        ]

    def body(m, carry):
        for c in range(tiles):
            for p in range(4):
                cut = slice(c * LANES, (c + 1) * LANES)
                sol_buf[c, m, pl.ds(p, q, stride=4), :] = x[m, p * q:(p + 1) * q, cut]
                res_buf[c, m, pl.ds(p, q, stride=4), :] = r[m, p * q:(p + 1) * q, cut]
        for copy in stores(m):
            copy.start()
        return carry

    lax.fori_loop(0, modes, body, 0)

    def drain(m, carry):
        for copy in stores(m):
            copy.wait()
        return carry

    lax.fori_loop(0, modes, drain, 0)


def strided(refs, p, q):
    return jnp.concatenate([ref[pl.ds(p, q, stride=4), :] for ref in refs], axis=1)


def stack_table(table):
    top = table.astype(bf16)
    low = (table - top.astype(np.float32)).astype(bf16)
    return np.concatenate([top, top, low], axis=0)


def shards(nc, ns, forcing, metric, jacobian, mode_scale):
    modes, rows, cols = forcing.shape
    block = np.kron(np.eye(cols // 4), SLOPES).astype(np.float32)
    grad, div = stack_table(block.T), stack_table(block)
    n, q, tiles = nc * ns, rows // 4, cols // LANES
    groups = GROUPS if modes % GROUPS == 0 else 1
    per = modes // groups
    slots = -(-(per + 2) // 8) * 8
    vm = pl.BlockSpec(memory_space=pltpu.VMEM)
    hbm = pl.BlockSpec(memory_space=pltpu.HBM)
    rounds, sums = (ITERS + 1) * groups, ITERS * groups
    field = pltpu.VMEM((modes, rows, cols), f32)
    split = pltpu.VMEM((tiles, modes, rows, LANES), f32)
    table = pltpu.VMEM(grad.shape, bf16)
    shape = jax.ShapeDtypeStruct(forcing.shape, f32)
    x, r = pl.pallas_call(
        functools.partial(kernel, nc, ns, modes, groups),
        out_shape=[shape] * 2,
        in_specs=[hbm] * 6,
        out_specs=[vm, vm],
        scratch_shapes=[
            field, field, field,
            pltpu.VMEM((modes + 2, rows, cols), f32),
            field,
            pltpu.VMEM((rows, cols), f32),
            pltpu.VMEM((rows, cols), f32),
            pltpu.VMEM((per * rows, 2 * cols), bf16),
            pltpu.VMEM((per * rows, cols), f32),
            pltpu.VMEM((2, slots, cols), f32),
            pltpu.VMEM((groups, 2, slots, cols), f32),
            pltpu.VMEM((rounds, 2, slots, cols), f32),
            pltpu.VMEM((rounds, 2, slots, cols), f32),
            pltpu.VMEM((rounds, 2, q, LANES), f32),
            pltpu.VMEM((rounds, 2, q, LANES), f32),
            pltpu.VMEM((rounds, 4, 1, LANES), f32),
            pltpu.VMEM((sums, 2, LANES), f32),
            pltpu.VMEM((sums, n, 2, LANES), f32),
            split,
            pltpu.VMEM((2, tiles, rows, LANES), f32),
            table, table,
            pltpu.SMEM((modes,), f32),
            pltpu.SemaphoreType.DMA((rounds, 8)),
            pltpu.SemaphoreType.DMA((rounds, 8)),
            pltpu.SemaphoreType.DMA((sums,)),
            pltpu.SemaphoreType.DMA((sums,)),
            pltpu.SemaphoreType.DMA((3, tiles)),
            pltpu.SemaphoreType.DMA((3,)),
        ],
        compiler_params=pltpu.CompilerParams(
            collective_id=0, has_side_effects=True, vmem_limit_bytes=41943040),
    )(*[pltpu.with_memory_space_constraint(v, pltpu.HBM) for v in (mode_scale, forcing, metric, jacobian, jnp.asarray(grad), jnp.asarray(div))])
    return pl.pallas_call(
        node_order,
        out_shape=[shape] * 2,
        in_specs=[vm, vm],
        out_specs=[hbm, hbm],
        scratch_shapes=[split, split, pltpu.SemaphoreType.DMA((2, tiles, modes))],
        compiler_params=pltpu.CompilerParams(vmem_limit_bytes=16 * 1024 * 1024),
    )(x, r)


def solution(mesh):
    placed = (P(None, "curve", "sub"), P("curve", "sub"), P("curve", "sub"), P())
    return jax.shard_map(
        functools.partial(shards, mesh.shape["curve"], mesh.shape["sub"]),
        mesh=mesh,
        in_specs=placed,
        out_specs=(P(None, "curve", "sub"), P(None, "curve", "sub")),
        check_vma=False,
    )
```

profile of v0, /device:TPU:0, one launch (start us, length us, event | category | flops | bytes accessed | tf_op | source)
XLA Modules:
  0.0 35.7 jit_solution(5842819093337775669)
XLA Ops:
  0.6 33.3 %shard_map.77 = (f32[12,96,256]{2,1,0:T(8,128)S(1)}, f32[12,96,256]{2,1,0:T(8,128)S(1)}) custom-call(f32[12]{0:T(128)} %scale_hbm.1, f32[12,96,256]{2,1,0:T(8,128)} %forcing_ref.1, f32[96,256]{1,0:T(8,128)} %metric_ref.1, f32[96,256]{1,0:T(8,128)} %jac_ref.1, bf16[768,256]{1,0:T(8,128)(2,1)} %constant.4.clone.grad_hbm, bf16[768,256]{1,0:T(8,128)(2,1)} %constant.5.clone.div_hbm), custom_call_target="tpu_custom_call" | custom-call | tf_op jit(solution)/shard_map/pallas_call | solution.py:425
  33.9 1.8 %shard_map.78 = (f32[12,96,256]{2,1,0:T(8,128)}, f32[12,96,256]{2,1,0:T(8,128)}) custom-call(f32[12,96,256]{2,1,0:T(8,128)S(1)} %get-tuple-element.4.x, f32[12,96,256]{2,1,0:T(8,128)S(1)} %get-tuple-element.5.r), custom_call_target="tpu_custom_call" | custom-call | tf_op jit(solution)/shard_map/pallas_call | solution.py:461
where the time goes:
time: 35.9 us; the launch traced here: 35.7 us
  Pallas kernels  35.1 us (98%)
  between operations  0.64 us (2%)
    pallas_call x1, Pallas kernels, shards(): pl.pallas_call(functools.partial(kernel, nc, ns, modes, groups), out_shap...  33.3 us
    pallas_call x1, Pallas kernels, shards(): pl.pallas_call(node_order, out_shape=[shape] * 2, in_specs=[vm, vm], out_...  1.8 us

commit v1 on v0

--- a/solution.py
+++ b/solution.py
@@ -11,6 +11,8 @@
 
 ITERS = 3
 GROUPS = 2
+SIGMA = 1.25
+LEVELS = 2 * ITERS
 UNROLL = True
 MESH = pl.DeviceIdType.MESH
 LANES = 128
@@ -49,8 +51,8 @@
 def kernel(
     nc, ns, modes, groups,
     scale_hbm, forcing_ref, metric_ref, jac_ref, grad_hbm, div_hbm,
-    x, r,
-    z, d, s, w, invp, mass, flux, zcat, gout, sums, coef,
+    v0, v1, v2, last, diag, coef,
+    w, invp, mass, flux, zcat, gout, sums,
     row_tx, row_rx, col_tx, col_rx, cor_rx, ar_tx, ar_rx,
     source, factors, grad_ref, div_ref, scale_ref,
     htx_sem, hrx_sem, atx_sem, arx_sem, in_sem, table_sem,
@@ -219,22 +221,8 @@
     scale_load.wait()
     grad_load.wait()
 
-    pad = (lax.broadcasted_iota(jnp.int32, (1, LANES), 1) >= per).astype(f32)
-    eye = lax.broadcasted_iota(jnp.int32, (slots, LANES), 0) == lax.broadcasted_iota(
-        jnp.int32, (slots, LANES), 1)
-
-    def update(it, g, m, slot, ww):
-        a, b = coef[g, 0, pl.ds(slot, 1), :], coef[g, 1, pl.ds(slot, 1), :]
-        zz = load(z, m)
-        if it > 1:
-            dd, ss = load(d, m), load(s, m)
-            zz = [u + b * v for u, v in zip(zz, dd)]
-            ww = [u + b * v for u, v in zip(ww, ss)]
-            xx = [u + a * v for u, v in zip(load(x, m), zz)]
-        else:
-            xx = [a * v for v in zz]
-        rr = [u - a * v for u, v in zip(load(r, m), ww)]
-        return zz, ww, xx, rr
+    basis = (v0, v1, v2)
+    span = sums.shape[0] // LEVELS
 
     def fill(slot, parts):
         v = jnp.concatenate(parts, axis=0)
@@ -247,25 +235,6 @@
         gout[...] = (
             jnp.dot(zcat[...], table_ref[:2 * cols, :], preferred_element_type=f32)
             + jnp.dot(zcat[:, :cols], table_ref[2 * cols:, :], preferred_element_type=f32))
-
-    old = [None] * groups
-
-    def coefficients(it, g):
-        k = it * groups + g
-        gathered = ar_rx.at[k, pl.ds(1, n - 1)]
-        pltpu.make_async_copy(gathered, gathered, arx_sem.at[k]).wait()
-        total = jnp.sum(ar_rx[k], axis=0)
-        rho, curve_sum = total[0:1] + pad, total[1:2] + pad
-        if it == 0:
-            mixing = jnp.zeros_like(rho)
-            step_len = rho / curve_sum
-        else:
-            mixing = rho / old[g][0]
-            step_len = rho / (curve_sum - mixing * rho / old[g][1])
-        for e, line in enumerate((step_len, mixing)):
-            tall = jnp.sum(jnp.where(eye, line, 0.0), axis=1, keepdims=True)
-            coef[g, e] = jnp.broadcast_to(tall, (slots, cols))
-        old[g] = (rho, step_len)
 
     for it in range(ITERS):
         for g in range(groups):
@@ -274,32 +243,25 @@
             merged = arrive(k)
             if it == 0 and g == 0:
                 for e in range(2):
-                    save(w, modes + e, assembled(k, modes + e, per + e, merged))
-            if it > 0:
-                coefficients(it - 1, g)
-
-            def first(slot, carry, it=it, g=g, k=k, base=base, merged=merged):
+                    save(diag, e, assembled(k, modes + e, per + e, merged))
+
+            def first(slot, carry, it=it, k=k, base=base, merged=merged):
                 m = base + slot
                 ww = assembled(k, m, slot, merged)
                 if it == 0:
-                    rr = ww
                     inv = [1.0 / (u + scale_ref[m] * v)
-                           for u, v in zip(load(w, modes), load(w, modes + 1))]
+                           for u, v in zip(load(diag, 0), load(diag, 1))]
                     save(invp, m, inv)
+                    zz = [u * v for u, v in zip(ww, inv)]
                 else:
-                    dd, ss, xx, rr = update(it, g, m, slot, ww)
-                    save(x, m, xx)
-                    save(d, m, dd)
-                    save(s, m, ss)
-                    inv = load(invp, m)
-                save(r, m, rr)
-                zz = [u * v for u, v in zip(rr, inv)]
-                save(z, m, zz)
+                    zz = [u * v - f32(SIGMA) * o
+                          for u, v, o in zip(ww, load(invp, m), load(basis[it - 1], m))]
+                save(basis[it], m, zz)
                 fill(slot, zz)
-                rz = [u * v for u, v in zip(rr, zz)]
+                rz = [u * v for u, v in zip(ww, zz)]
                 rho = (rz[0] + rz[3]) * 0.5 + (rz[1] + rz[2])
                 rho = jnp.where(on_edge, rho * 0.5, rho)
-                sums[0, pl.ds(slot, 1), :] = jnp.sum(rho, axis=0, keepdims=True)
+                sums[pl.ds(2 * it * span + m, 1), :] = jnp.sum(rho, axis=0, keepdims=True)
                 f = load2(flux)
                 fg = [f[a] * combo(SLOPES[a], zz) * scale_ref[m] for a in range(4)]
                 ms = load2(mass)
@@ -317,57 +279,95 @@
             lax.fori_loop(0, per, second, 0, unroll=UNROLL)
             multiply(div_ref)
 
-            def third(slot, carry, k=k, base=base):
+            def third(slot, carry, it=it, k=k, base=base):
                 m = base + slot
-                zz = load(z, m)
+                zz = load(basis[it], m)
                 h = [u + gout[pl.ds(pl.multiple_of(slot * rows + p * q, q), q), :]
                      for p, u in enumerate(load(w, m))]
                 zh = zz[0] * h[0] + zz[1] * h[1] + zz[2] * h[2] + zz[3] * h[3]
-                sums[1, pl.ds(slot, 1), :] = jnp.sum(zh, axis=0, keepdims=True)
+                sums[pl.ds((2 * it + 1) * span + m, 1), :] = jnp.sum(zh, axis=0, keepdims=True)
                 return pack(k + groups, m, slot, h, carry)
 
             tops = lax.fori_loop(0, per, third, (zero, zero), unroll=UNROLL)
             send(k + groups, tops)
-            for e in range(2):
-                part = jnp.sum(sums[e], axis=1, keepdims=True)
-                line = jnp.sum(jnp.where(eye, part, 0.0), axis=0, keepdims=True)
-                ar_tx[k, e:e + 1, :] = line
-                ar_rx[k, 0, e:e + 1, :] = line
-
-            def spread(offset, carry, k=k):
-                pltpu.make_async_remote_copy(
-                    src_ref=ar_tx.at[k], dst_ref=ar_rx.at[k, offset],
-                    send_sem=atx_sem.at[k], recv_sem=arx_sem.at[k],
-                    device_id=place(offset), device_id_type=MESH).start()
-                return carry
-
-            lax.fori_loop(1, n, spread, 0, unroll=True if n <= 32 else 1)
+
+    total_rows = sums.shape[0]
+    wide = ar_tx.shape[1]
+    eye = lax.broadcasted_iota(jnp.int32, (total_rows, wide), 0) == lax.broadcasted_iota(
+        jnp.int32, (total_rows, wide), 1)
+    part = jnp.sum(sums[...], axis=1, keepdims=True)
+    line = jnp.sum(jnp.where(eye, part, 0.0), axis=0, keepdims=True)
+    ar_tx[...] = line
+    ar_rx[0:1, :] = line
+
+    def spread(offset, carry):
+        pltpu.make_async_remote_copy(
+            src_ref=ar_tx, dst_ref=ar_rx.at[pl.ds(offset, 1)],
+            send_sem=atx_sem, recv_sem=arx_sem,
+            device_id=place(offset), device_id_type=MESH).start()
+        return carry
+
+    lax.fori_loop(1, n, spread, 0, unroll=True if n <= 32 else 1)
 
     for g in range(groups):
         k = ITERS * groups + g
         merged = arrive(k)
-        coefficients(ITERS - 1, g)
-
-        def last(slot, carry, g=g, k=k, merged=merged):
+
+        def finish(slot, carry, g=g, k=k, merged=merged):
             m = g * per + slot
-            _, _, xx, rr = update(ITERS, g, m, slot, assembled(k, m, slot, merged))
-            save(x, m, xx)
-            save(r, m, rr)
+            save(last, m, assembled(k, m, slot, merged))
             return carry
 
-        lax.fori_loop(0, per, last, 0, unroll=UNROLL)
+        lax.fori_loop(0, per, finish, 0, unroll=UNROLL)
+
+    gathered = ar_rx.at[pl.ds(1, n - 1)]
+    pltpu.make_async_copy(gathered, gathered, arx_sem).wait()
+    total = jnp.sum(ar_rx[...], axis=0, keepdims=True)
+    solve(total, span, coef)
 
     for k in range((ITERS + 1) * groups):
         for copy in halo_copies(k):
             copy.wait_send()
-    for k in range(ITERS * groups):
-        sent = ar_rx.at[k, pl.ds(1, n - 1)]
-        pltpu.make_async_copy(sent, sent, atx_sem.at[k]).wait()
-
-
-def node_order(x, r, sol_ref, res_ref, sol_buf, res_buf, sem):
-    modes, rows, cols = x.shape
+    pltpu.make_async_copy(gathered, gathered, atx_sem).wait()
+
+
+def solve(total, span, coef):
+    wide = total.shape[1]
+    live = lax.broadcasted_iota(jnp.int32, (1, wide), 1) < coef.shape[1]
+    b0, a0, b1, a1, b2, a2 = [
+        jnp.where(live, total if e == 0 else pltpu.roll(total, wide - e * span, 1), 1.0)
+        for e in range(LEVELS)]
+    sigma = f32(SIGMA)
+    n1 = a0 - sigma * b0
+    n2 = b1 - sigma * n1
+    n3 = a1 - sigma * n2
+    g02 = n3 + sigma * n2
+    l1, l2 = b1 / a0, g02 / a0
+    d1 = a1 - l1 * b1
+    e12 = b2 - l1 * g02
+    l3 = e12 / d1
+    d2 = a2 - l2 * g02 - l3 * e12
+    y1 = n1 - l1 * b0
+    y2 = n2 - l2 * b0 - l3 * y1
+    c2 = y2 / d2
+    c1 = y1 / d1 - l3 * c2
+    c0 = b0 / a0 - l1 * c1 - l2 * c2
+    spot = (lax.broadcasted_iota(jnp.int32, (coef.shape[1], wide), 0)
+            == lax.broadcasted_iota(jnp.int32, (coef.shape[1], wide), 1))
+    for e, line in enumerate((c0, c1, c2, 1.0 - sigma * c0, c0 + sigma * c1)):
+        tall = jnp.sum(jnp.where(spot, line, 0.0), axis=1, keepdims=True)
+        coef[e] = jnp.broadcast_to(tall, coef.shape[1:])
+
+
+def node_order(
+    scale_hbm, v0, v1, v2, last, diag, coef, sol_ref, res_ref,
+    sol_buf, res_buf, scale_ref, sem, scale_sem,
+):
+    modes, rows, cols = v0.shape
     q, tiles = rows // 4, cols // LANES
+    scale_load = pltpu.make_async_copy(scale_hbm, scale_ref, scale_sem)
+    scale_load.start()
+    scale_load.wait()
 
     def stores(m):
         return [
@@ -378,11 +378,17 @@
         ]
 
     def body(m, carry):
-        for c in range(tiles):
-            for p in range(4):
-                cut = slice(c * LANES, (c + 1) * LANES)
-                sol_buf[c, m, pl.ds(p, q, stride=4), :] = x[m, p * q:(p + 1) * q, cut]
-                res_buf[c, m, pl.ds(p, q, stride=4), :] = r[m, p * q:(p + 1) * q, cut]
+        c0, c1, c2, k0, k1 = [coef[e, pl.ds(m, 1), :] for e in range(5)]
+        for p in range(4):
+            cut = slice(p * q, (p + 1) * q)
+            a, b, c = v0[m, cut, :], v1[m, cut, :], v2[m, cut, :]
+            x = c0 * a + c1 * b + c2 * c
+            weight = diag[0, cut, :] + scale_ref[m] * diag[1, cut, :]
+            r = weight * (k0 * a - k1 * b - c1 * c) - c2 * last[m, cut, :]
+            for t in range(tiles):
+                lanes = slice(t * LANES, (t + 1) * LANES)
+                sol_buf[t, m, pl.ds(p, q, stride=4), :] = x[:, lanes]
+                res_buf[t, m, pl.ds(p, q, stride=4), :] = r[:, lanes]
         for copy in stores(m):
             copy.start()
         return carry
@@ -417,41 +423,43 @@
     slots = -(-(per + 2) // 8) * 8
     vm = pl.BlockSpec(memory_space=pltpu.VMEM)
     hbm = pl.BlockSpec(memory_space=pltpu.HBM)
-    rounds, sums = (ITERS + 1) * groups, ITERS * groups
+    rounds = (ITERS + 1) * groups
+    span = -(-modes // 8) * 8
+    wide = -(-LEVELS * span // LANES) * LANES
     field = pltpu.VMEM((modes, rows, cols), f32)
     split = pltpu.VMEM((tiles, modes, rows, LANES), f32)
     table = pltpu.VMEM(grad.shape, bf16)
     shape = jax.ShapeDtypeStruct(forcing.shape, f32)
-    x, r = pl.pallas_call(
+    built = pl.pallas_call(
         functools.partial(kernel, nc, ns, modes, groups),
-        out_shape=[shape] * 2,
+        out_shape=[shape] * 4 + [
+            jax.ShapeDtypeStruct((2, rows, cols), f32),
+            jax.ShapeDtypeStruct((5, span, cols), f32)],
         in_specs=[hbm] * 6,
-        out_specs=[vm, vm],
+        out_specs=[vm] * 6,
         scratch_shapes=[
-            field, field, field,
             pltpu.VMEM((modes + 2, rows, cols), f32),
             field,
             pltpu.VMEM((rows, cols), f32),
             pltpu.VMEM((rows, cols), f32),
             pltpu.VMEM((per * rows, 2 * cols), bf16),
             pltpu.VMEM((per * rows, cols), f32),
-            pltpu.VMEM((2, slots, cols), f32),
-            pltpu.VMEM((groups, 2, slots, cols), f32),
+            pltpu.VMEM((LEVELS * span, cols), f32),
             pltpu.VMEM((rounds, 2, slots, cols), f32),
             pltpu.VMEM((rounds, 2, slots, cols), f32),
             pltpu.VMEM((rounds, 2, q, LANES), f32),
             pltpu.VMEM((rounds, 2, q, LANES), f32),
             pltpu.VMEM((rounds, 4, 1, LANES), f32),
-            pltpu.VMEM((sums, 2, LANES), f32),
-            pltpu.VMEM((sums, n, 2, LANES), f32),
+            pltpu.VMEM((1, wide), f32),
+            pltpu.VMEM((n, wide), f32),
             split,
             pltpu.VMEM((2, tiles, rows, LANES), f32),
             table, table,
             pltpu.SMEM((modes,), f32),
             pltpu.SemaphoreType.DMA((rounds, 8)),
             pltpu.SemaphoreType.DMA((rounds, 8)),
-            pltpu.SemaphoreType.DMA((sums,)),
-            pltpu.SemaphoreType.DMA((sums,)),
+            pltpu.SemaphoreType.DMA,
+            pltpu.SemaphoreType.DMA,
             pltpu.SemaphoreType.DMA((3, tiles)),
             pltpu.SemaphoreType.DMA((3,)),
         ],
@@ -461,11 +469,13 @@
     return pl.pallas_call(
         node_order,
         out_shape=[shape] * 2,
-        in_specs=[vm, vm],
+        in_specs=[hbm] + [vm] * 6,
         out_specs=[hbm, hbm],
-        scratch_shapes=[split, split, pltpu.SemaphoreType.DMA((2, tiles, modes))],
+        scratch_shapes=[
+            split, split, pltpu.SMEM((modes,), f32),
+            pltpu.SemaphoreType.DMA((2, tiles, modes)), pltpu.SemaphoreType.DMA],
         compiler_params=pltpu.CompilerParams(vmem_limit_bytes=16 * 1024 * 1024),
-    )(x, r)
+    )(pltpu.with_memory_space_constraint(mode_scale, pltpu.HBM), *built)
 
 
 def solution(mesh):

time: 35.9 us -> 34.6 us (0.964)
  Pallas kernels: 35.1 us -> 33.8 us
    pallas_call x1, Pallas kernels: 33.3 us -> 31.3 us  [shards(): pl.pallas_call(functools.partial(kernel, nc, ns, modes, groups), out_shap...]
    pallas_call x1, Pallas kernels: 1.8 us -> 2.5 us  [shards(): pl.pallas_call(node_order, out_shape=[shape] * 2, in_specs=[hbm] + [vm] *...]
where the time goes in v1:
time: 34.6 us; the launch traced here: 34.4 us
  Pallas kernels  33.8 us (98%)
  between operations  0.64 us (2%)
    pallas_call x1, Pallas kernels, shards(): pl.pallas_call(functools.partial(kernel, nc, ns, modes, groups), out_shap...  31.3 us
    pallas_call x1, Pallas kernels, shards(): pl.pallas_call(node_order, out_shape=[shape] * 2, in_specs=[hbm] + [vm] *...  2.5 us

profile of v1, /device:TPU:0, one launch (start us, length us, event | category | flops | bytes accessed | tf_op | source)
XLA Modules:
  0.0 34.4 jit_solution(1040022372945110545)
XLA Ops:
  0.6 31.3 %shard_map.77 = (f32[12,96,256]{2,1,0:T(8,128)S(1)}, f32[12,96,256]{2,1,0:T(8,128)S(1)}, f32[12,96,256]{2,1,0:T(8,128)S(1)}, f32[12,96,256]{2,1,0:T(8,128)S(1)},...) custom-call(f32[12]{0:T(128)} %scale_hbm.3, f32[12,96,256]{2,1,0:T(8,128)} %forcing_ref.1, f32[96,256]{1,0:T(8,128)} %metric_ref.1, ...), custom_call_target="tpu_custom_call" | custom-call | tf_op jit(solution)/shard_map/pallas_call | solution.py:433
  31.9 2.5 %shard_map.78 = (f32[12,96,256]{2,1,0:T(8,128)}, f32[12,96,256]{2,1,0:T(8,128)}) custom-call(f32[12]{0:T(128)} %scale_hbm.3, f32[12,96,256]{2,1,0:T(8,128)S(1)} %get-tuple-element.8.v0, f32[12,96,256]{2,1,0:T(8,128)S(1)} %get-tuple-element.9.v1, f32[12,96,256]{2,1,0:T(8,128)S(1)} %get-tuple-element.10.v2, f32[12,96,256]{2,1,0:T(8,128)S(1)} %get-tuple-element.11.last, ...), custom_call_target="tpu_custom_call" | custom-call | tf_op jit(solution)/shard_map/pallas_call | solution.py:469

commit v2 on v1

v2 whole, which is shorter than its diff:
```python
import functools
import math

import jax
import jax.numpy as jnp
import numpy as np
from jax import lax
from jax.experimental import pallas as pl
from jax.experimental.pallas import tpu as pltpu
from jax.sharding import PartitionSpec as P

ITERS = 3
GROUPS = 2
SIGMA = 1.25
SUMS = 2 * ITERS
UNROLL = True
OUT_UNROLL = 4
MESH = pl.DeviceIdType.MESH
LANES = 128
f32 = jnp.float32
bf16 = jnp.bfloat16


def gll_tables():
    points = np.array([-1.0, -1.0 / math.sqrt(5.0), 1.0 / math.sqrt(5.0), 1.0])
    weights = np.array([1.0 / 6.0, 5.0 / 6.0, 5.0 / 6.0, 1.0 / 6.0])
    factor = np.array(
        [np.prod([points[j] - points[m] for m in range(4) if m != j]) for j in range(4)]
    )
    slopes = np.zeros((4, 4))
    for i in range(4):
        for j in range(4):
            if i != j:
                slopes[i, j] = factor[i] / (factor[j] * (points[i] - points[j]))
        slopes[i, i] = sum((1.0 / (points[i] - points[m]) for m in range(4) if m != i))
    return (slopes, weights)


SLOPES, WEIGHTS = gll_tables()


def combo(coefs, parts):
    total = None
    for c, v in zip(coefs, parts):
        if abs(c) < 1e-12:
            continue
        term = v * f32(c)
        total = term if total is None else total + term
    return total


def apply_line(table, v):
    phase = lax.broadcasted_iota(jnp.int32, (1, LANES), 1) % 4
    total = None
    for d in range(-3, 4):
        coef = jnp.zeros((1, LANES), f32)
        for p in range(4):
            if 0 <= p + d < 4 and abs(table[p, p + d]) > 1e-12:
                coef = jnp.where(phase == p, f32(table[p, p + d]), coef)
        moved = v if d == 0 else pltpu.roll(v, (LANES - d) % LANES, 1)
        total = coef * moved if total is None else total + coef * moved
    return total


def stiff_line(flux, v):
    return apply_line(SLOPES.T, flux * apply_line(SLOPES, v))


def kernel(
    nc, ns, modes, groups,
    scale_hbm, forcing_ref, metric_ref, jac_ref, grad_hbm, div_hbm,
    v0, v1, v2, last, diag, coef, edge_row, edge_col,
    w, invp, mass, flux, zcat, gout, sums,
    row_e, col_e, row_d, col_d, row_m, row_i, col_m, col_i, row_fix, col_fix, row_k, col_k,
    row_c, col_c,
    row_tx, row_rx, col_tx, col_rx, cor_rx, ar_tx, ar_rx,
    source, factors, grad_ref, div_ref, scale_ref,
    htx_sem, hrx_sem, atx_sem, arx_sem, in_sem, table_sem,
):
    rows, cols = metric_ref.shape
    q = rows // 4
    n = nc * ns
    half = cols - LANES
    tiles = cols // LANES
    per = modes // groups
    slots = row_tx.shape[2]
    loads, sources = [], []
    for c in range(tiles):
        cut = pl.ds(c * LANES, LANES)
        loads += [
            pltpu.make_async_copy(jac_ref.at[:, cut], factors.at[0, c], in_sem.at[0, c]),
            pltpu.make_async_copy(metric_ref.at[:, cut], factors.at[1, c], in_sem.at[1, c]),
        ]
        sources.append(
            pltpu.make_async_copy(forcing_ref.at[:, :, cut], source.at[c], in_sem.at[2, c]))
    div_load = pltpu.make_async_copy(div_hbm, div_ref, table_sem.at[0])
    grad_load = pltpu.make_async_copy(grad_hbm, grad_ref, table_sem.at[1])
    scale_load = pltpu.make_async_copy(scale_hbm, scale_ref, table_sem.at[2])
    for copy in loads + sources + [scale_load]:
        copy.start()

    me_c, me_s = lax.axis_index("curve"), lax.axis_index("sub")
    me = me_c * ns + me_s
    up, down = lax.rem(me_c + nc - 1, nc), lax.rem(me_c + 1, nc)
    left, right = lax.rem(me_s + ns - 1, ns), lax.rem(me_s + 1, ns)

    def place(offset):
        target = lax.rem(me + offset, n)
        return (target // ns, lax.rem(target, ns))

    barrier = pltpu.get_barrier_semaphore()

    def greet(offset, carry):
        pl.semaphore_signal(barrier, inc=1, device_id=place(offset), device_id_type=MESH)
        return carry

    lax.fori_loop(1, n, greet, 0)

    def iota(shape, axis):
        return lax.broadcasted_iota(jnp.int32, shape, axis)

    def ways(shape):
        at = iota(shape, 1)
        return (at % 4 == 3) & (at != cols - 1), (at % 4 == 0) & (at != 0)

    lane_full = iota((q, cols), 1)
    lane = iota((q, LANES), 1)
    row_at = iota((q, cols), 0)
    edge_at = iota((q, LANES), 0)
    phase = lane_full % 4
    on_edge = (phase == 0) | (phase == 3)
    inside = (lane_full != 0) & (lane_full != cols - 1)

    def load(ref, m):
        return [ref[m, p * q:(p + 1) * q, :] for p in range(4)]

    def save(ref, m, parts):
        for p in range(4):
            ref[m, p * q:(p + 1) * q, :] = parts[p]

    def load2(ref):
        return [ref[p * q:(p + 1) * q, :] for p in range(4)]

    def join_cols(t, shape):
        take_next, take_prev = ways(shape)
        return t + jnp.where(
            take_next, pltpu.roll(t, cols - 1, 1),
            jnp.where(take_prev, pltpu.roll(t, 1, 1), 0.0))

    def join_rows(c):
        ph = lane % 4
        after = pltpu.roll(pltpu.roll(c, LANES - (LANES - 3), 1), q - 1, 0)
        before = pltpu.roll(pltpu.roll(c, LANES - 3, 1), 1, 0)
        return c + jnp.where((ph == 3) & (edge_at != q - 1), after,
                             jnp.where((ph == 0) & (edge_at != 0), before, 0.0))

    def pack(rows_ref, m, slot, h, tops):
        lo, hi = tops
        rows_ref[0, pl.ds(slot, 1), :] = h[0][0:1, :]
        rows_ref[1, pl.ds(slot, 1), :] = h[3][q - 1:q, :]
        save(w, m, joined(h))
        for p in range(4):
            at = 4 * slot + p
            lo = jnp.where(lane == at, pltpu.roll(h[p][:, :LANES], at, 1), lo)
            hi = jnp.where(lane == at, pltpu.roll(h[p][:, half:], at + 1, 1), hi)
        return lo, hi

    def halo_copies(k):
        plan = [
            (row_tx.at[k, 0], row_rx.at[k, 1], (up, me_s)),
            (row_tx.at[k, 1], row_rx.at[k, 0], (down, me_s)),
            (col_tx.at[k, 0, pl.ds(0, 1)], cor_rx.at[k, 3], (up, left)),
            (col_tx.at[k, 1, pl.ds(0, 1)], cor_rx.at[k, 2], (up, right)),
            (col_tx.at[k, 0, pl.ds(q - 1, 1)], cor_rx.at[k, 1], (down, left)),
            (col_tx.at[k, 1, pl.ds(q - 1, 1)], cor_rx.at[k, 0], (down, right)),
            (col_tx.at[k, 0], col_rx.at[k, 1], (me_c, left)),
            (col_tx.at[k, 1], col_rx.at[k, 0], (me_c, right)),
        ]
        return [
            pltpu.make_async_remote_copy(
                src_ref=src, dst_ref=dst, send_sem=htx_sem.at[k, e], recv_sem=hrx_sem.at[k, e],
                device_id=where, device_id_type=MESH)
            for e, (src, dst, where) in enumerate(plan)
        ]

    def send(k):
        for copy in halo_copies(k):
            copy.start()

    ends = ((0, 0), (q - 1, 3))
    tall = iota((slots, LANES), 0)
    wide_lane = iota((slots, LANES), 1)

    def to_rows(line, p0, target):
        found = jnp.where(wide_lane == 4 * tall + p0, line, 0.0)
        found = jnp.sum(found, axis=1, keepdims=True)
        return jnp.where(wide_lane == target, found, 0.0)

    def to_cols(block, p0, target):
        at = wide_lane == 4 * tall + p0
        spread = jnp.broadcast_to(block[:, target:target + 1], (slots, LANES))
        return jnp.sum(jnp.where(at, spread, 0.0), axis=0, keepdims=True)

    def at_sides(lo, hi):
        middle = [jnp.zeros((slots, LANES), f32)] * (tiles - 2)
        return jnp.concatenate([lo] + middle + [hi], axis=1)

    def side_tile(block, side):
        return block[:, half:] if side else block[:, :LANES]

    def arrive(k):
        for copy in halo_copies(k):
            copy.wait_recv()
        ph = iota((1, LANES), 1) % 4
        merged = []
        for side in range(2):
            above, below = cor_rx[k, side], cor_rx[k, 2 + side]
            above = jnp.where(ph == 0, pltpu.roll(above, LANES - 3, 1), 0.0)
            below = jnp.where(ph == 3, pltpu.roll(below, 3, 1), 0.0)
            c = col_rx[k, side]
            merged.append(
                c + jnp.where(edge_at == 0, above, 0.0) + jnp.where(edge_at == q - 1, below, 0.0))
        on_rows, on_cols = [], []
        for end, (at, p0) in enumerate(ends):
            t = join_cols(row_tx[k, end] + row_rx[k, end], (slots, cols))
            on_rows.append(t + at_sides(
                to_rows(merged[0][at:at + 1, :], p0, 0),
                to_rows(merged[1][at:at + 1, :], p0, LANES - 1)))
        for side in range(2):
            c = col_tx[k, side] + merged[side]
            for end, (at, p0) in enumerate(ends):
                line = to_cols(side_tile(row_rx[k, end], side), p0, (LANES - 1) * side)
                c = c + jnp.where(edge_at == at, line, 0.0)
            on_cols.append(c)
        return on_rows, on_cols

    def fixed(m):
        t = load(w, m)
        for p in range(4):
            pieces = [t[p][:, e * LANES:(e + 1) * LANES] for e in range(tiles)]
            for side, e in ((0, 0), (1, tiles - 1)):
                value = pltpu.roll(col_fix[side], LANES - 4 * m - p, 1)[:, 0:1]
                pieces[e] = pieces[e] + value * col_k[side, p]
            t[p] = jnp.concatenate(pieces, axis=1)
            blocks = [t[p][:8, :], t[p][8:q - 8, :], t[p][q - 8:, :]]
            for end, (at, p0) in enumerate(ends):
                line = row_fix[end, p, pl.ds(m, 1), :]
                spot = 7 * end if p != p0 else 1 + 5 * end
                blocks[2 * end] = blocks[2 * end] + jnp.where(row_at[:8, :] == spot, line, 0.0)
            t[p] = jnp.concatenate(blocks, axis=0)
        return t

    def joined(h):
        t0 = h[0] + jnp.where(row_at == 0, 0.0, pltpu.roll(h[3], 1, 0))
        t3 = h[3] + jnp.where(row_at == q - 1, 0.0, pltpu.roll(h[0], q - 1, 0))
        return [join_cols(t, (q, cols)) for t in (t0, h[1], h[2], t3)]

    def clear(parts):
        keep = [inside] * 4
        keep[0] = inside & (row_at != 0)
        keep[3] = inside & (row_at != q - 1)
        return [jnp.where(k, u, 0.0) for k, u in zip(keep, parts)]

    edge_w, mid_w = f32(1.0 / 6.0), f32(5.0 / 6.0)
    grid_lane = jnp.where(on_edge, edge_w, mid_w)
    mw, fw = [], []
    for copy in loads:
        copy.wait()
    for p in range(4):
        grid_w = grid_lane * (edge_w if p in (0, 3) else mid_w)
        mw.append(strided([factors.at[0, c] for c in range(tiles)], p, q) * grid_w)
        fw.append(strided([factors.at[1, c] for c in range(tiles)], p, q) * grid_w)
        mass[p * q:(p + 1) * q, :] = mw[p]
        flux[p * q:(p + 1) * q, :] = fw[p]
    zero = jnp.zeros((q, LANES), f32)
    tops = pack(row_tx.at[0], modes, modes, mw, (zero, zero))
    squared = SLOPES * SLOPES

    def per_line(fn, block):
        return jnp.concatenate(
            [fn(block[:, e * LANES:(e + 1) * LANES], e) for e in range(tiles)], axis=1)

    lap = [combo(squared[:, a], fw) + per_line(lambda v, e: apply_line(squared.T, v), fw[a])
           for a in range(4)]
    tops = pack(row_tx.at[0], modes + 1, modes + 1, lap, tops)
    for copy in sources:
        copy.wait()
    grad_load.start()
    div_load.start()

    def start_body(m, carry):
        h = [strided([source.at[c, m] for c in range(tiles)], p, q)
             * mass[p * q:(p + 1) * q, :] for p in range(4)]
        return pack(row_tx.at[0], m, m, h, carry)

    tops = lax.fori_loop(0, modes, start_body, tops, unroll=2)
    for side in range(2):
        col_tx[0, side] = join_rows(tops[side])
    pl.semaphore_wait(barrier, n - 1)
    send(0)
    scale_load.wait()

    basis = (v0, v1, v2)
    span = sums.shape[0] // SUMS
    scale_rows = jnp.zeros((slots, LANES), f32)
    scale_lanes = jnp.zeros((1, LANES), f32)
    lane_one = iota((1, LANES), 1)
    for m in range(modes):
        scale_rows = jnp.where(tall == m, scale_ref[m], scale_rows)
        scale_lanes = jnp.where(lane_one // 4 == m, scale_ref[m], scale_lanes)
    scale_rows = jnp.concatenate([scale_rows] * tiles, axis=1)

    ffull, mfull = load2(flux), load2(mass)
    line_lane = iota((1, cols), 1)
    not_corner = (line_lane != 0) & (line_lane != cols - 1)
    for end, (at, p0) in enumerate(ends):
        cut = [f[at:at + 1, :] for f in ffull]
        row_c[end, 0:1, :] = cut[p0]
        row_c[end, 1:2, :] = mfull[p0][at:at + 1, :]
        row_c[end, 2:3, :] = jnp.where(not_corner, combo(SLOPES[:, p0] ** 2, cut), 0.0)
        for p in range(4):
            far = p if p != p0 else 3 - p0
            row_k[end, p:p + 1, :] = join_cols(
                combo(SLOPES[:, p0] * SLOPES[:, far], cut), (1, cols))
    for side in range(2):
        fc, mc, dc = zero, zero, zero
        reach = []
        for p in range(4):
            f = side_tile(ffull[p], side)
            base = half and (LANES - 4) * side
            cells = [jnp.broadcast_to(f[:, base + b:base + b + 1], (q, LANES)) for b in range(4)]
            b0 = 3 * side
            mass_cell = side_tile(mfull[p], side)[:, base + b0:base + b0 + 1]
            mine = lane % 4 == p
            fc = jnp.where(mine, cells[b0], fc)
            mc = jnp.where(mine, mass_cell, mc)
            dc = jnp.where(mine, combo(SLOPES[:, b0] ** 2, cells), dc)
            block = zero
            for b in range(4):
                if b != b0:
                    hit = lane == base + b
                    if b == 3 - b0:
                        hit = hit | (lane == base + b + 1 - 2 * side)
                    block = jnp.where(hit, combo(SLOPES[:, b0] * SLOPES[:, b], cells), block)
            reach.append(block)
        col_k[side, 0] = reach[0] + jnp.where(edge_at == 0, 0.0, pltpu.roll(reach[3], 1, 0))
        col_k[side, 1], col_k[side, 2] = reach[1], reach[2]
        col_k[side, 3] = reach[3] + jnp.where(
            edge_at == q - 1, 0.0, pltpu.roll(reach[0], q - 1, 0))
        for at, p0 in ends:
            dc = jnp.where((edge_at == at) & (lane % 4 == p0), 0.0, dc)
        col_c[side, 0], col_c[side, 1], col_c[side, 2] = fc, mc, dc

    def fill(b, slot, parts):
        v = jnp.concatenate(parts, axis=0)
        top = v.astype(bf16)
        at = pl.ds(pl.multiple_of(slot * rows, rows), rows)
        zcat[b, at, :cols] = top
        zcat[b, at, cols:] = (v - top.astype(f32)).astype(bf16)

    def multiply(b, table_ref):
        gout[b] = (
            jnp.dot(zcat[b], table_ref[:2 * cols, :], preferred_element_type=f32)
            + jnp.dot(zcat[b, :, :cols], table_ref[2 * cols:, :], preferred_element_type=f32))

    def build(it):
        tops = (zero, zero)
        for b in range(groups):
            base = b * per

            def first(slot, carry, b=b, base=base):
                m = base + slot
                t = load(w, m) if it == 0 else fixed(m)
                if it == 0:
                    inv = clear([1.0 / (u + scale_ref[m] * v)
                                 for u, v in zip(load(diag, 0), load(diag, 1))])
                    save(invp, m, inv)
                    zz = [u * v for u, v in zip(t, inv)]
                else:
                    zz = [u * v - f32(SIGMA) * o
                          for u, v, o in zip(t, load(invp, m), load(basis[it - 1], m))]
                save(basis[it], m, zz)
                fill(b, slot, zz)
                rz = [u * v for u, v in zip(t, zz)]
                rho = (rz[0] + rz[3]) * 0.5 + (rz[1] + rz[2])
                rho = jnp.where(on_edge, rho * 0.5, rho)
                sums[pl.ds(2 * it * span + m, 1), :] = jnp.sum(rho, axis=0, keepdims=True)
                f = load2(flux)
                fg = [f[a] * combo(SLOPES[a], zz) * scale_ref[m] for a in range(4)]
                ms = load2(mass)
                save(w, m, [ms[a] * zz[a] + combo(SLOPES[:, a], fg) for a in range(4)])
                return carry

            lax.fori_loop(0, per, first, 0, unroll=True)
            if it == 0 and b == 0:
                grad_load.wait()
                div_load.wait()
            multiply(b, grad_ref)

            def second(slot, carry, b=b, base=base):
                grad = gout[b, pl.ds(pl.multiple_of(slot * rows, rows), rows), :]
                fill(b, slot, [flux[...] * grad * scale_ref[base + slot]])
                return carry

            lax.fori_loop(0, per, second, 0, unroll=True)
            multiply(b, div_ref)

            def third(slot, carry, b=b, base=base):
                m = base + slot
                zz = load(basis[it], m)
                h = [u + gout[b, pl.ds(pl.multiple_of(slot * rows + p * q, q), q), :]
                     for p, u in enumerate(load(w, m))]
                zh = zz[0] * h[0] + zz[1] * h[1] + zz[2] * h[2] + zz[3] * h[3]
                sums[pl.ds((2 * it + 1) * span + m, 1), :] = jnp.sum(zh, axis=0, keepdims=True)
                return pack(row_e, m, m, h, carry)

            tops = lax.fori_loop(0, per, third, tops, unroll=True)
        col_e[0], col_e[1] = tops

    row_weight = jnp.where((line_lane % 4 == 0) | (line_lane % 4 == 3), 0.25, 0.5).astype(f32)
    corner = ((edge_at == 0) & (lane % 4 == 0)) | ((edge_at == q - 1) & (lane % 4 == 3))
    col_weight = jnp.where((lane % 4 == 0) | (lane % 4 == 3), 0.25, 0.5).astype(f32)
    col_weight = jnp.where(corner, 0.0, col_weight)
    own_slot = wide_lane // 4 == tall

    def fold(e, on_rows, on_cols):
        at = slice(e * span, e * span + slots)
        sums[at, :] = sums[at, :] + (on_rows[0] + on_rows[1])
        line = jnp.sum(on_cols[0] + on_cols[1], axis=0, keepdims=True)
        sums[at, :LANES] = sums[at, :LANES] + jnp.where(own_slot, line, 0.0)

    def step(it):
        on_rows, on_cols = arrive(it)
        row_now, col_now, row_s, col_s = [], [], [], []
        for i in range(2):
            if it == 0:
                t = on_rows[i]
                weight = t[modes:modes + 1, :] + scale_rows * t[modes + 1:modes + 2, :]
                row_m[i], row_i[i] = weight, 1.0 / weight
                c = on_cols[i]
                md, ld = zero, zero
                for p in range(4):
                    a, b = 4 * modes + p, 4 * modes + 4 + p
                    md = jnp.where(lane % 4 == p, c[:, a:a + 1], md)
                    ld = jnp.where(lane % 4 == p, c[:, b:b + 1], ld)
                weight = md + scale_lanes * ld
                col_m[i], col_i[i] = weight, 1.0 / weight
            r, c = on_rows[i] * row_i[i], on_cols[i] * col_i[i]
            if it > 0:
                r, c = r - f32(SIGMA) * row_d[it - 1, i], c - f32(SIGMA) * col_d[it - 1, i]
            row_d[it, i], col_d[it, i] = r, c
            row_now.append(r)
            col_now.append(c)
            row_s.append(per_line(
                lambda v, e, i=i: stiff_line(row_c[i, 0:1, e * LANES:(e + 1) * LANES], v), r))
            col_s.append(stiff_line(col_c[i, 0], c))
        row_out, col_out = [], []
        for end, (at, p0) in enumerate(ends):
            across = at_sides(
                to_rows(col_s[0][at:at + 1, :], p0, 0),
                to_rows(col_s[1][at:at + 1, :], p0, LANES - 1))
            r = row_now[end]
            row_out.append(
                row_e[end] + row_c[end, 1:2, :] * r
                + scale_rows * (row_c[end, 2:3, :] * r + row_s[end] + across))
        for side in range(2):
            total = col_s[side] + col_c[side, 2] * col_now[side]
            for end, (at, p0) in enumerate(ends):
                line = to_cols(side_tile(row_s[end], side), p0, (LANES - 1) * side)
                total = total + jnp.where((edge_at == at) & (lane % 4 == p0), line, 0.0)
            col_out.append(
                col_e[side] + col_c[side, 1] * col_now[side] + scale_lanes * total)
        for i in range(2):
            row_tx[it + 1, i] = row_out[i]
            col_tx[it + 1, i] = join_rows(col_out[i])
        if it < ITERS - 1:
            send(it + 1)
        fold(2 * it,
             [row_weight * u * v for u, v in zip(row_now, on_rows)],
             [col_weight * u * v for u, v in zip(col_now, on_cols)])
        fold(2 * it + 1,
             [u * (a + b) for u, a, b in zip(row_now, [row_e[0], row_e[1]], row_out)],
             [jnp.where(corner, 0.0, u * (a + b))
              for u, a, b in zip(col_now, [col_e[0], col_e[1]], col_out)])
        lines.append(reduce_sums(it))
        if it == ITERS - 1:
            spread_sums()
            send(it + 1)
        for i, (at, p0) in enumerate(ends):
            col_fix[i] = scale_lanes * col_now[i]
            for p in range(4):
                row_fix[i, p] = scale_rows * row_now[i] * row_k[i, p:p + 1, :]

    wide = ar_tx.shape[1]
    gathered = ar_rx.at[pl.ds(1, n - 1)]
    lines = []

    def reduce_sums(it):
        base = 2 * it * span
        eye = iota((2 * span, wide), 0) + base == iota((2 * span, wide), 1)
        part = jnp.sum(sums[base:base + 2 * span, :], axis=1, keepdims=True)
        return jnp.sum(jnp.where(eye, part, 0.0), axis=0, keepdims=True)

    def spread_sums():
        line = sum(lines)
        ar_tx[...] = line
        ar_rx[0:1, :] = line

        def spread(offset, carry):
            pltpu.make_async_remote_copy(
                src_ref=ar_tx, dst_ref=ar_rx.at[pl.ds(offset, 1)],
                send_sem=atx_sem, recv_sem=arx_sem,
                device_id=place(offset), device_id_type=MESH).start()
            return carry

        lax.fori_loop(1, n, spread, 0, unroll=True if n <= 32 else 1)

    sums[...] = jnp.zeros_like(sums)
    for e in range(2):
        save(diag, e, load(w, modes + e))
    for it in range(ITERS):
        build(it)
        step(it)

    def finish(m, carry):
        save(last, m, clear(fixed(m)))
        return carry

    lax.fori_loop(0, modes, finish, 0, unroll=2)
    on_rows, on_cols = arrive(ITERS)
    pltpu.make_async_copy(gathered, gathered, arx_sem).wait()
    total = jnp.sum(ar_rx[...], axis=0, keepdims=True)
    solve(total, span, coef)
    on_lanes = [
        jnp.sum(jnp.where(own_slot, coef[e, :slots, :LANES], 0.0), axis=0, keepdims=True)
        for e in range(5)]
    for i in range(2):
        for ref, given, prior, weight, (c0, c1, c2, k0, k1) in (
                (edge_row, on_rows[i], row_d, row_m[i], [coef[e, :slots, :] for e in range(5)]),
                (edge_col, on_cols[i], col_d, col_m[i], on_lanes)):
            a, b, c = prior[0, i], prior[1, i], prior[2, i]
            ref[0, i] = c0 * a + c1 * b + c2 * c
            ref[1, i] = weight * (k0 * a - k1 * b - c1 * c) - c2 * given

    for k in range(ITERS + 1):
        for copy in halo_copies(k):
            copy.wait_send()
    pltpu.make_async_copy(gathered, gathered, atx_sem).wait()


def solve(total, span, coef):
    wide = total.shape[1]
    live = lax.broadcasted_iota(jnp.int32, (1, wide), 1) < coef.shape[1]
    b0, a0, b1, a1, b2, a2 = [
        jnp.where(live, total if e == 0 else pltpu.roll(total, wide - e * span, 1), 1.0)
        for e in range(SUMS)]
    sigma = f32(SIGMA)
    n1 = a0 - sigma * b0
    n2 = b1 - sigma * n1
    n3 = a1 - sigma * n2
    g02 = n3 + sigma * n2
    l1, l2 = b1 / a0, g02 / a0
    d1 = a1 - l1 * b1
    e12 = b2 - l1 * g02
    l3 = e12 / d1
    d2 = a2 - l2 * g02 - l3 * e12
    y1 = n1 - l1 * b0
    y2 = n2 - l2 * b0 - l3 * y1
    c2 = y2 / d2
    c1 = y1 / d1 - l3 * c2
    c0 = b0 / a0 - l1 * c1 - l2 * c2
    spot = (lax.broadcasted_iota(jnp.int32, (coef.shape[1], wide), 0)
            == lax.broadcasted_iota(jnp.int32, (coef.shape[1], wide), 1))
    for e, line in enumerate((c0, c1, c2, 1.0 - sigma * c0, c0 + sigma * c1)):
        tall = jnp.sum(jnp.where(spot, line, 0.0), axis=1, keepdims=True)
        coef[e] = jnp.broadcast_to(tall, coef.shape[1:])


def node_order(
    scale_hbm, v0, v1, v2, last, diag, coef, edge_row, edge_col, sol_ref, res_ref,
    sol_buf, res_buf, scale_ref, sem, scale_sem,
):
    modes, rows, cols = v0.shape
    q, tiles = rows // 4, cols // LANES
    scale_load = pltpu.make_async_copy(scale_hbm, scale_ref, scale_sem)
    scale_load.start()
    scale_load.wait()

    lane = lax.broadcasted_iota(jnp.int32, (q, LANES), 1)

    def stores(m):
        return [
            pltpu.make_async_copy(
                buf.at[c, m], out.at[m, :, pl.ds(c * LANES, LANES)], sem.at[k, c, m])
            for k, (buf, out) in enumerate(((sol_buf, sol_ref), (res_buf, res_ref)))
            for c in range(tiles)
        ]

    def body(m, carry):
        c0, c1, c2, k0, k1 = [coef[e, pl.ds(m, 1), :] for e in range(5)]
        for p in range(4):
            cut = slice(p * q, (p + 1) * q)
            a, b, c = v0[m, cut, :], v1[m, cut, :], v2[m, cut, :]
            x = c0 * a + c1 * b + c2 * c
            weight = diag[0, cut, :] + scale_ref[m] * diag[1, cut, :]
            r = weight * (k0 * a - k1 * b - c1 * c) - c2 * last[m, cut, :]
            for field, (buf, whole) in enumerate(((sol_buf, x), (res_buf, r))):
                for t in range(tiles):
                    piece = whole[:, t * LANES:(t + 1) * LANES]
                    for side, own in ((0, 0), (1, tiles - 1)):
                        if t == own:
                            spot = (LANES - 1) * side
                            line = pltpu.roll(
                                edge_col[field, side], spot + LANES - 4 * m - p, 1)
                            piece = piece + jnp.where(lane == spot, line, 0.0)
                    buf[t, m, pl.ds(p, q, stride=4), :] = piece
        for field, buf in enumerate((sol_buf, res_buf)):
            for end, at in ((0, 0), (1, rows - 1)):
                line = edge_row[field, end, pl.ds(m, 1), :]
                for t in range(tiles):
                    buf[t, m, at:at + 1, :] = line[:, t * LANES:(t + 1) * LANES]
        for copy in stores(m):
            copy.start()
        return carry

    lax.fori_loop(0, modes, body, 0, unroll=OUT_UNROLL)

    def drain(m, carry):
        for copy in stores(m):
            copy.wait()
        return carry

    lax.fori_loop(0, modes, drain, 0)


def strided(refs, p, q):
    return jnp.concatenate([ref[pl.ds(p, q, stride=4), :] for ref in refs], axis=1)


def stack_table(table):
    top = table.astype(bf16)
    low = (table - top.astype(np.float32)).astype(bf16)
    return np.concatenate([top, top, low], axis=0)


def shards(nc, ns, forcing, metric, jacobian, mode_scale):
    modes, rows, cols = forcing.shape
    block = np.kron(np.eye(cols // 4), SLOPES).astype(np.float32)
    grad, div = stack_table(block.T), stack_table(block)
    n, q, tiles = nc * ns, rows // 4, cols // LANES
    groups = GROUPS if modes % GROUPS == 0 else 1
    per = modes // groups
    slots = -(-(modes + 2) // 8) * 8
    vm = pl.BlockSpec(memory_space=pltpu.VMEM)
    hbm = pl.BlockSpec(memory_space=pltpu.HBM)
    rounds = ITERS + 1
    span = slots
    wide = -(-SUMS * span // LANES) * LANES
    field = pltpu.VMEM((modes, rows, cols), f32)
    split = pltpu.VMEM((tiles, modes, rows, LANES), f32)
    table = pltpu.VMEM(grad.shape, bf16)
    shape = jax.ShapeDtypeStruct(forcing.shape, f32)

    def on_rows(*lead):
        return pltpu.VMEM((*lead, slots, cols), f32)

    def on_cols(*lead):
        return pltpu.VMEM((*lead, q, LANES), f32)

    built = pl.pallas_call(
        functools.partial(kernel, nc, ns, modes, groups),
        out_shape=[shape] * 4 + [
            jax.ShapeDtypeStruct((2, rows, cols), f32),
            jax.ShapeDtypeStruct((5, span, cols), f32),
            jax.ShapeDtypeStruct((2, 2, slots, cols), f32),
            jax.ShapeDtypeStruct((2, 2, q, LANES), f32)],
        in_specs=[hbm] * 6,
        out_specs=[vm] * 8,
        scratch_shapes=[
            pltpu.VMEM((modes + 2, rows, cols), f32),
            field,
            pltpu.VMEM((rows, cols), f32),
            pltpu.VMEM((rows, cols), f32),
            pltpu.VMEM((groups, per * rows, 2 * cols), bf16),
            pltpu.VMEM((groups, per * rows, cols), f32),
            pltpu.VMEM((SUMS * span, cols), f32),
            on_rows(2), on_cols(2),
            on_rows(ITERS, 2), on_cols(ITERS, 2),
            on_rows(2), on_rows(2), on_cols(2), on_cols(2),
            on_rows(2, 4), on_cols(2),
            pltpu.VMEM((2, 8, cols), f32),
            on_cols(2, 4),
            pltpu.VMEM((2, 8, cols), f32),
            on_cols(2, 3),
            on_rows(rounds, 2), on_rows(rounds, 2),
            on_cols(rounds, 2), on_cols(rounds, 2),
            pltpu.VMEM((rounds, 4, 1, LANES), f32),
            pltpu.VMEM((1, wide), f32),
            pltpu.VMEM((n, wide), f32),
            split,
            pltpu.VMEM((2, tiles, rows, LANES), f32),
            table, table,
            pltpu.SMEM((modes,), f32),
            pltpu.SemaphoreType.DMA((rounds, 8)),
            pltpu.SemaphoreType.DMA((rounds, 8)),
            pltpu.SemaphoreType.DMA,
            pltpu.SemaphoreType.DMA,
            pltpu.SemaphoreType.DMA((3, tiles)),
            pltpu.SemaphoreType.DMA((3,)),
        ],
        compiler_params=pltpu.CompilerParams(
            collective_id=0, has_side_effects=True, vmem_limit_bytes=41943040),
    )(*[pltpu.with_memory_space_constraint(v, pltpu.HBM) for v in (mode_scale, forcing, metric, jacobian, jnp.asarray(grad), jnp.asarray(div))])
    return pl.pallas_call(
        node_order,
        out_shape=[shape] * 2,
        in_specs=[hbm] + [vm] * 8,
        out_specs=[hbm, hbm],
        scratch_shapes=[
            split, split, pltpu.SMEM((modes,), f32),
            pltpu.SemaphoreType.DMA((2, tiles, modes)), pltpu.SemaphoreType.DMA],
        compiler_params=pltpu.CompilerParams(vmem_limit_bytes=16 * 1024 * 1024),
    )(pltpu.with_memory_space_constraint(mode_scale, pltpu.HBM), *built)


def solution(mesh):
    placed = (P(None, "curve", "sub"), P("curve", "sub"), P("curve", "sub"), P())
    return jax.shard_map(
        functools.partial(shards, mesh.shape["curve"], mesh.shape["sub"]),
        mesh=mesh,
        in_specs=placed,
        out_specs=(P(None, "curve", "sub"), P(None, "curve", "sub")),
        check_vma=False,
    )
```

time: 34.6 us -> 30.8 us (0.89)
  Pallas kernels: 33.8 us -> 30 us
    pallas_call x1, Pallas kernels: 31.3 us -> 27.3 us  [shards(): pl.pallas_call(functools.partial(kernel, nc, ns, modes, groups), out_shap...]
where the time goes in v2:
time: 30.8 us; the launch traced here: 30.6 us
  Pallas kernels  30 us (97%)
  between operations  0.64 us (2%)
    pallas_call x1, Pallas kernels, shards(): pl.pallas_call(functools.partial(kernel, nc, ns, modes, groups), out_shap...  27.3 us
    pallas_call x1, Pallas kernels, shards(): pl.pallas_call(node_order, out_shape=[shape] * 2, in_specs=[hbm] + [vm] *...  2.67 us

profile of v2, /device:TPU:0, one launch (start us, length us, event | category | flops | bytes accessed | tf_op | source)
XLA Modules:
  0.0 30.6 jit_solution(13896362003888655612)
XLA Ops:
  0.6 27.3 %shard_map.77 = (f32[12,96,256]{2,1,0:T(8,128)S(1)}, f32[12,96,256]{2,1,0:T(8,128)S(1)}, f32[12,96,256]{2,1,0:T(8,128)S(1)}, f32[12,96,256]{2,1,0:T(8,128)S(1)},...) custom-call(f32[12]{0:T(128)} %scale_hbm.3, ...), custom_call_target="tpu_custom_call" | custom-call | tf_op jit(solution)/shard_map/pallas_call | solution.py:670
  27.9 2.7 %shard_map.78 = (f32[12,96,256]{2,1,0:T(8,128)}, f32[12,96,256]{2,1,0:T(8,128)}) custom-call(f32[12]{0:T(128)} %scale_hbm.3, f32[12,96,256]{2,1,0:T(8,128)S(1)} %get-tuple-element.10.v0, f32[12,96,256]{2,1,0:T(8,128)S(1)} %get-tuple-element.11.v1, f32[12,96,256]{2,1,0:T(8,128)S(1)} %get-tuple-element.12.v2, f32[12,96,256]{2,1,0:T(8,128)S(1)} %get-tuple-element.13.last, ...), custom_call_target="tpu_custom_call" | custom-call | tf_op jit(solution)/shard_map/pallas_call | solution.py:714

commit v3 on v2

--- a/solution.py
+++ b/solution.py
@@ -62,8 +62,22 @@
     return total
 
 
-def stiff_line(flux, v):
-    return apply_line(SLOPES.T, flux * apply_line(SLOPES, v))
+def bands(flux):
+    out = []
+    for d in range(-3, 4):
+        table = np.zeros((4, 4))
+        for p in range(4):
+            if 0 <= p + d < 4:
+                table[p] = SLOPES[:, p] * SLOPES[:, p + d]
+        out.append(apply_line(table, flux))
+    return out
+
+
+def stiff_line(band, v):
+    total = band(3) * v
+    for d in (-3, -2, -1, 1, 2, 3):
+        total = total + band(3 + d) * pltpu.roll(v, (LANES - d) % LANES, 1)
+    return total
 
 
 def kernel(
@@ -114,7 +128,7 @@
         pl.semaphore_signal(barrier, inc=1, device_id=place(offset), device_id_type=MESH)
         return carry
 
-    lax.fori_loop(1, n, greet, 0)
+    lax.fori_loop(1, n, greet, 0, unroll=True if n <= 32 else 1)
 
     def iota(shape, axis):
         return lax.broadcasted_iota(jnp.int32, shape, axis)
@@ -309,15 +323,19 @@
         scale_rows = jnp.where(tall == m, scale_ref[m], scale_rows)
         scale_lanes = jnp.where(lane_one // 4 == m, scale_ref[m], scale_lanes)
     scale_rows = jnp.concatenate([scale_rows] * tiles, axis=1)
+    coef[5] = scale_rows
 
     ffull, mfull = load2(flux), load2(mass)
     line_lane = iota((1, cols), 1)
     not_corner = (line_lane != 0) & (line_lane != cols - 1)
     for end, (at, p0) in enumerate(ends):
         cut = [f[at:at + 1, :] for f in ffull]
-        row_c[end, 0:1, :] = cut[p0]
-        row_c[end, 1:2, :] = mfull[p0][at:at + 1, :]
-        row_c[end, 2:3, :] = jnp.where(not_corner, combo(SLOPES[:, p0] ** 2, cut), 0.0)
+        pieces = [bands(cut[p0][:, e * LANES:(e + 1) * LANES]) for e in range(tiles)]
+        for d in range(7):
+            row_c[end, d:d + 1, :] = jnp.concatenate([b[d] for b in pieces], axis=1)
+        row_c[end, 3:4, :] = row_c[end, 3:4, :] + jnp.where(
+            not_corner, combo(SLOPES[:, p0] ** 2, cut), 0.0)
+        row_c[end, 7:8, :] = mfull[p0][at:at + 1, :]
         for p in range(4):
             far = p if p != p0 else 3 - p0
             row_k[end, p:p + 1, :] = join_cols(
@@ -349,7 +367,9 @@
             edge_at == q - 1, 0.0, pltpu.roll(reach[0], q - 1, 0))
         for at, p0 in ends:
             dc = jnp.where((edge_at == at) & (lane % 4 == p0), 0.0, dc)
-        col_c[side, 0], col_c[side, 1], col_c[side, 2] = fc, mc, dc
+        for d, band in enumerate(bands(fc)):
+            col_c[side, d] = band + dc if d == 3 else band
+        col_c[side, 7] = mc
 
     def fill(b, slot, parts):
         v = jnp.concatenate(parts, axis=0)
@@ -452,8 +472,9 @@
             row_now.append(r)
             col_now.append(c)
             row_s.append(per_line(
-                lambda v, e, i=i: stiff_line(row_c[i, 0:1, e * LANES:(e + 1) * LANES], v), r))
-            col_s.append(stiff_line(col_c[i, 0], c))
+                lambda v, e, i=i: stiff_line(
+                    lambda d: row_c[i, d:d + 1, e * LANES:(e + 1) * LANES], v), r))
+            col_s.append(stiff_line(lambda d, i=i: col_c[i, d], c))
         row_out, col_out = [], []
         for end, (at, p0) in enumerate(ends):
             across = at_sides(
@@ -461,15 +482,14 @@
                 to_rows(col_s[1][at:at + 1, :], p0, LANES - 1))
             r = row_now[end]
             row_out.append(
-                row_e[end] + row_c[end, 1:2, :] * r
-                + scale_rows * (row_c[end, 2:3, :] * r + row_s[end] + across))
+                row_e[end] + row_c[end, 7:8, :] * r + scale_rows * (row_s[end] + across))
         for side in range(2):
-            total = col_s[side] + col_c[side, 2] * col_now[side]
+            total = col_s[side]
             for end, (at, p0) in enumerate(ends):
                 line = to_cols(side_tile(row_s[end], side), p0, (LANES - 1) * side)
                 total = total + jnp.where((edge_at == at) & (lane % 4 == p0), line, 0.0)
             col_out.append(
-                col_e[side] + col_c[side, 1] * col_now[side] + scale_lanes * total)
+                col_e[side] + col_c[side, 7] * col_now[side] + scale_lanes * total)
         for i in range(2):
             row_tx[it + 1, i] = row_out[i]
             col_tx[it + 1, i] = join_rows(col_out[i])
@@ -506,7 +526,8 @@
         ar_tx[...] = line
         ar_rx[0:1, :] = line
 
-        def spread(offset, carry):
+        def spread(i, carry):
+            offset = jnp.where(i % 2 == 1, (i + 1) // 2, n - i // 2)
             pltpu.make_async_remote_copy(
                 src_ref=ar_tx, dst_ref=ar_rx.at[pl.ds(offset, 1)],
                 send_sem=atx_sem, recv_sem=arx_sem,
@@ -577,14 +598,11 @@
 
 
 def node_order(
-    scale_hbm, v0, v1, v2, last, diag, coef, edge_row, edge_col, sol_ref, res_ref,
-    sol_buf, res_buf, scale_ref, sem, scale_sem,
+    v0, v1, v2, last, diag, coef, edge_row, edge_col, sol_ref, res_ref,
+    sol_buf, res_buf, sem,
 ):
     modes, rows, cols = v0.shape
     q, tiles = rows // 4, cols // LANES
-    scale_load = pltpu.make_async_copy(scale_hbm, scale_ref, scale_sem)
-    scale_load.start()
-    scale_load.wait()
 
     lane = lax.broadcasted_iota(jnp.int32, (q, LANES), 1)
 
@@ -597,12 +615,12 @@
         ]
 
     def body(m, carry):
-        c0, c1, c2, k0, k1 = [coef[e, pl.ds(m, 1), :] for e in range(5)]
+        c0, c1, c2, k0, k1, scale = [coef[e, pl.ds(m, 1), :] for e in range(6)]
         for p in range(4):
             cut = slice(p * q, (p + 1) * q)
             a, b, c = v0[m, cut, :], v1[m, cut, :], v2[m, cut, :]
             x = c0 * a + c1 * b + c2 * c
-            weight = diag[0, cut, :] + scale_ref[m] * diag[1, cut, :]
+            weight = diag[0, cut, :] + scale * diag[1, cut, :]
             r = weight * (k0 * a - k1 * b - c1 * c) - c2 * last[m, cut, :]
             for field, (buf, whole) in enumerate(((sol_buf, x), (res_buf, r))):
                 for t in range(tiles):
@@ -671,7 +689,7 @@
         functools.partial(kernel, nc, ns, modes, groups),
         out_shape=[shape] * 4 + [
             jax.ShapeDtypeStruct((2, rows, cols), f32),
-            jax.ShapeDtypeStruct((5, span, cols), f32),
+            jax.ShapeDtypeStruct((6, span, cols), f32),
             jax.ShapeDtypeStruct((2, 2, slots, cols), f32),
             jax.ShapeDtypeStruct((2, 2, q, LANES), f32)],
         in_specs=[hbm] * 6,
@@ -691,7 +709,7 @@
             pltpu.VMEM((2, 8, cols), f32),
             on_cols(2, 4),
             pltpu.VMEM((2, 8, cols), f32),
-            on_cols(2, 3),
+            on_cols(2, 8),
             on_rows(rounds, 2), on_rows(rounds, 2),
             on_cols(rounds, 2), on_cols(rounds, 2),
             pltpu.VMEM((rounds, 4, 1, LANES), f32),
@@ -714,13 +732,12 @@
     return pl.pallas_call(
         node_order,
         out_shape=[shape] * 2,
-        in_specs=[hbm] + [vm] * 8,
+        in_specs=[vm] * 8,
         out_specs=[hbm, hbm],
         scratch_shapes=[
-            split, split, pltpu.SMEM((modes,), f32),
-            pltpu.SemaphoreType.DMA((2, tiles, modes)), pltpu.SemaphoreType.DMA],
+            split, split, pltpu.SemaphoreType.DMA((2, tiles, modes))],
         compiler_params=pltpu.CompilerParams(vmem_limit_bytes=16 * 1024 * 1024),
-    )(pltpu.with_memory_space_constraint(mode_scale, pltpu.HBM), *built)
+    )(*built)
 
 
 def solution(mesh):

time: 30.8 us -> 29.1 us (0.945)
  Pallas kernels: 30 us -> 28.3 us
    pallas_call x1, Pallas kernels: 27.3 us -> 26.3 us  [shards(): pl.pallas_call(functools.partial(kernel, nc, ns, modes, groups), out_shap...]
    pallas_call x1, Pallas kernels: 2.67 us -> 2 us  [shards(): pl.pallas_call(node_order, out_shape=[shape] * 2, in_specs=[vm] * 8, out_...]
where the time goes in v3:
time: 29.1 us; the launch traced here: 29 us
  Pallas kernels  28.3 us (97%)
  between operations  0.64 us (2%)
    pallas_call x1, Pallas kernels, shards(): pl.pallas_call(functools.partial(kernel, nc, ns, modes, groups), out_shap...  26.3 us
    pallas_call x1, Pallas kernels, shards(): pl.pallas_call(node_order, out_shape=[shape] * 2, in_specs=[vm] * 8, out_...  2 us

profile of v3, /device:TPU:0, one launch (start us, length us, event | category | flops | bytes accessed | tf_op | source)
XLA Modules:
  0.0 29.0 jit_solution(16817977190956705872)
XLA Ops:
  0.6 26.3 %shard_map.77 = (f32[12,96,256]{2,1,0:T(8,128)S(1)}, f32[12,96,256]{2,1,0:T(8,128)S(1)}, f32[12,96,256]{2,1,0:T(8,128)S(1)}, f32[12,96,256]{2,1,0:T(8,128)S(1)},...) custom-call(f32[12]{0:T(128)} %scale_hbm.1, ...), custom_call_target="tpu_custom_call" | custom-call | tf_op jit(solution)/shard_map/pallas_call | solution.py:688
  27.0 2.0 %shard_map.78 = (f32[12,96,256]{2,1,0:T(8,128)}, f32[12,96,256]{2,1,0:T(8,128)}) custom-call(f32[12,96,256]{2,1,0:T(8,128)S(1)} %get-tuple-element.10.v0, f32[12,96,256]{2,1,0:T(8,128)S(1)} %get-tuple-element.11.v1, f32[12,96,256]{2,1,0:T(8,128)S(1)} %get-tuple-element.12.v2, f32[12,96,256]{2,1,0:T(8,128)S(1)} %get-tuple-element.13.last, ...), custom_call_target="tpu_custom_call" | custom-call | tf_op jit(solution)/shard_map/pallas_call | solution.py:732

commit v4 on v3

--- a/solution.py
+++ b/solution.py
@@ -181,12 +181,12 @@
 
     def halo_copies(k):
         plan = [
-            (row_tx.at[k, 0], row_rx.at[k, 1], (up, me_s)),
-            (row_tx.at[k, 1], row_rx.at[k, 0], (down, me_s)),
             (col_tx.at[k, 0, pl.ds(0, 1)], cor_rx.at[k, 3], (up, left)),
             (col_tx.at[k, 1, pl.ds(0, 1)], cor_rx.at[k, 2], (up, right)),
             (col_tx.at[k, 0, pl.ds(q - 1, 1)], cor_rx.at[k, 1], (down, left)),
             (col_tx.at[k, 1, pl.ds(q - 1, 1)], cor_rx.at[k, 0], (down, right)),
+            (row_tx.at[k, 0], row_rx.at[k, 1], (up, me_s)),
+            (row_tx.at[k, 1], row_rx.at[k, 0], (down, me_s)),
             (col_tx.at[k, 0], col_rx.at[k, 1], (me_c, left)),
             (col_tx.at[k, 1], col_rx.at[k, 0], (me_c, right)),
         ]
@@ -548,6 +548,9 @@
         return carry
 
     lax.fori_loop(0, modes, finish, 0, unroll=2)
+    for k in range(ITERS):
+        for copy in halo_copies(k):
+            copy.wait_send()
     on_rows, on_cols = arrive(ITERS)
     pltpu.make_async_copy(gathered, gathered, arx_sem).wait()
     total = jnp.sum(ar_rx[...], axis=0, keepdims=True)
@@ -563,9 +566,8 @@
             ref[0, i] = c0 * a + c1 * b + c2 * c
             ref[1, i] = weight * (k0 * a - k1 * b - c1 * c) - c2 * given
 
-    for k in range(ITERS + 1):
-        for copy in halo_copies(k):
-            copy.wait_send()
+    for copy in halo_copies(ITERS):
+        copy.wait_send()
     pltpu.make_async_copy(gathered, gathered, atx_sem).wait()
 
 

time: 29.1 us -> 29.1 us (level)
  no operation moved by 1% of the time
where the time goes in v4:
time: 29.1 us; the launch traced here: 28.9 us
  Pallas kernels  28.3 us (97%)
  between operations  0.64 us (2%)
    pallas_call x1, Pallas kernels, shards(): pl.pallas_call(functools.partial(kernel, nc, ns, modes, groups), out_shap...  26.3 us
    pallas_call x1, Pallas kernels, shards(): pl.pallas_call(node_order, out_shape=[shape] * 2, in_specs=[vm] * 8, out_...  2 us

profile of v4, /device:TPU:0, one launch (start us, length us, event | category | flops | bytes accessed | tf_op | source)
XLA Modules:
  0.0 28.9 jit_solution(16647397161308866449)
XLA Ops:
  0.6 26.3 %shard_map.77 = (f32[12,96,256]{2,1,0:T(8,128)S(1)}, f32[12,96,256]{2,1,0:T(8,128)S(1)}, f32[12,96,256]{2,1,0:T(8,128)S(1)}, f32[12,96,256]{2,1,0:T(8,128)S(1)},...) custom-call(f32[12]{0:T(128)} %scale_hbm.1, ...), custom_call_target="tpu_custom_call" | custom-call | tf_op jit(solution)/shard_map/pallas_call | solution.py:690
  26.9 2.0 %shard_map.78 = (f32[12,96,256]{2,1,0:T(8,128)}, f32[12,96,256]{2,1,0:T(8,128)}) custom-call(f32[12,96,256]{2,1,0:T(8,128)S(1)} %get-tuple-element.10.v0, f32[12,96,256]{2,1,0:T(8,128)S(1)} %get-tuple-element.11.v1, f32[12,96,256]{2,1,0:T(8,128)S(1)} %get-tuple-element.12.v2, f32[12,96,256]{2,1,0:T(8,128)S(1)} %get-tuple-element.13.last, ...), custom_call_target="tpu_custom_call" | custom-call | tf_op jit(solution)/shard_map/pallas_call | solution.py:734
